TPU v7x, 32 devices: a whole 2x2x4 slice. The times are simulated.
32 devices in a mesh: panel: 8 (over z, y), obs: 4 (over x, core).
Axes of the slice: x: 2, y: 2, z: 4, core: 2. Of those that a mesh axis runs over, the one named last changes fastest.
Arguments:
- flow_blocks: bfloat16 [1024, 4, 1280], P('panel'), may hold values from -6 to 6
- interp_weights: bfloat16 [32, 128, 512], P(('panel', 'obs')), may hold values from -0.25 to 0.25
- donor_owner: int32 [4096, 1], P(('panel', 'obs')), may hold values from 0 to 7; in each aligned block of 128 rows (0 to 127, 128 to 255, ...) at most 24 rows name the same one
- donor_block: int32 [4096], P(('panel', 'obs')), may hold values from 0 to 127
- panel_normals: float32 [3, 4096], P(None, ('panel', 'obs')), may hold values from -3 to 3
- panel_points: float32 [3, 4096], P(None, ('panel', 'obs')), may hold values from -1 to 1
- observer_points: float32 [3, 1024], P(None, 'obs'), may hold values from -12 to 12, as said below
Outputs:
- pressure: float32 [128, 1024], P('panel', 'obs')
Inputs may be any that keep to these rules, and one draw needn't show every extreme that they name: `donor_owner`: within the rows of one device, no owner index is named by more than 24 rows; some devices' rows name one owner exactly 24 times. `observer_points`: every observer lies between 6 and 12 from the anchor.
All inputs are finite; a program needn't handle non-finite values.
Results may differ from a plain program's by a relative error of at most 0.0003.
Values may be sent and summed in bfloat16 or wider, within the bound.
A program may use at most 64 MiB of HBM per device.

v0:
```python
import functools
import math

import jax
import jax.numpy as jnp
from jax import lax
from jax.experimental import pallas as pl
from jax.experimental.pallas import tpu as pltpu
from jax.sharding import PartitionSpec as P

NV = 5
NT = 256
HARM = 64


KAPPA = 0.5


def fourier_table(samples, orders):
    sample_ids = jnp.arange(samples, dtype=jnp.int32)
    harmonic = jnp.arange(1, orders + 1, dtype=jnp.int32)
    wrapped = sample_ids[:, None] * harmonic[None, :] % samples
    angles = wrapped.astype(jnp.float32) * (2.0 * math.pi / samples)
    factor = 2.0 / samples
    return jnp.concatenate([factor * jnp.cos(angles), -factor * jnp.sin(angles)], axis=1)


def spectra_of(values, normals, transform, samples):
    panels = values.shape[0]
    fields = values.reshape(panels, NV, samples)
    density = 1.0 + fields[:, 0]
    velocity = fields[:, 1:4]
    pressure_pert = fields[:, 4]
    normal_vec = jnp.transpose(normals)[:, :, None]
    normal_flow = jnp.sum(velocity * normal_vec, axis=1)
    mass_flux = density * normal_flow
    loading = pressure_pert[:, None, :] * normal_vec + mass_flux[:, None, :] * velocity
    series = jnp.concatenate([mass_flux[:, None, :], loading], axis=1)
    return jnp.einsum("pct,tk->cpk", series, transform, precision=lax.Precision.HIGHEST)


GROUP = 8
SLOT = 8


def sin_cos(angle):
    turns = jnp.floor(angle * (2.0 / math.pi) + 0.5)
    reduced = angle - turns * 1.5703125
    reduced = reduced - turns * 4.837512969970703125e-4
    reduced = reduced - turns * 7.54978995489188216e-8
    square = reduced * reduced
    sine = ((-1.9515295891e-4 * square + 8.3321608736e-3) * square - 1.6666654611e-1) * square * reduced + reduced
    cosine = ((2.443315711809948e-5 * square - 1.388731625493765e-3) * square + 4.166664568298827e-2) * square * square - 0.5 * square + 1.0
    quadrant = turns.astype(jnp.int32)
    swap = (quadrant & 1) == 1
    out_sin = jnp.where(swap, cosine, sine)
    out_cos = jnp.where(swap, sine, cosine)
    out_sin = jnp.where((quadrant & 2) == 2, -out_sin, out_sin)
    out_cos = jnp.where(((quadrant + 1) & 2) == 2, -out_cos, out_cos)
    return out_sin, out_cos


def split_hi_lo(array):
    high = array.astype(jnp.bfloat16).astype(jnp.float32)
    return high, array - high


def geometry(points, observers, cos_ref, sin_ref):
    offsets = [observers[i : i + 1, :] - points[:, i : i + 1] for i in range(3)]
    squared = offsets[0] * offsets[0] + offsets[1] * offsets[1] + offsets[2] * offsets[2]
    distance = jnp.sqrt(squared)
    inverse = 1.0 / distance
    weight = inverse * (1.0 / (4.0 * math.pi))
    far = [offset * (inverse * weight) for offset in offsets]
    near = [term * inverse for term in far]
    slots = near + far + [weight, jnp.zeros_like(weight)]
    high, low = split_hi_lo(jnp.concatenate(slots, axis=0))
    right = jnp.concatenate([high, high, low, low], axis=0).astype(jnp.bfloat16)
    sine, cosine = sin_cos(KAPPA * distance)
    twice = 2.0 * cosine
    past_cos, past_sin = jnp.ones_like(cosine), jnp.zeros_like(sine)
    for order in range(8):
        cos_ref[order] = cosine
        sin_ref[order] = sine
        cosine, past_cos = twice * cosine - past_cos, cosine
        sine, past_sin = twice * sine - past_sin, sine
    return right


def amplitude(left, right, out_ref):
    lanes = lax.broadcasted_iota(jnp.int32, (1, left.shape[1]), 1) % GROUP
    rows = left.shape[0]
    masked = [left * (lanes == y).astype(jnp.float32).astype(jnp.bfloat16) for y in range(GROUP)]
    stacked = jnp.concatenate(masked, axis=0)
    out_ref[...] = jnp.dot(stacked, right, preferred_element_type=jnp.float32)


def accumulate(amp_ref, cos_ref, sin_ref, acc_ref):
    rows, observers = acc_ref.shape
    orders = rows // 2
    blocks = orders // 8
    for half in range(observers // 128):
        lane = pl.ds(half * 128, 128)
        acc_re = [acc_ref[pl.ds(8 * b, 8), lane] for b in range(blocks)]
        acc_im = [acc_ref[pl.ds(orders + 8 * b, 8), lane] for b in range(blocks)]
        for y in range(GROUP):
            cosine = cos_ref[:, y, lane]
            sine = sin_ref[:, y, lane]
            step_cos = cos_ref[7, pl.ds(y, 1), lane]
            step_sin = sin_ref[7, pl.ds(y, 1), lane]
            twice = 2.0 * step_cos
            past_cos = past_sin = None
            for b in range(blocks):
                amp_re = amp_ref[pl.ds(y * rows + 8 * b, 8), lane]
                amp_im = amp_ref[pl.ds(y * rows + orders + 8 * b, 8), lane]
                acc_re[b] = acc_re[b] + (amp_re * cosine + amp_im * sine)
                acc_im[b] = acc_im[b] + (amp_im * cosine - amp_re * sine)
                if b == 0:
                    next_cos = cosine * step_cos - sine * step_sin
                    next_sin = sine * step_cos + cosine * step_sin
                else:
                    next_cos = twice * cosine - past_cos
                    next_sin = twice * sine - past_sin
                past_cos, past_sin, cosine, sine = cosine, sine, next_cos, next_sin
        for b in range(blocks):
            acc_ref[pl.ds(8 * b, 8), lane] = acc_re[b]
            acc_ref[pl.ds(orders + 8 * b, 8), lane] = acc_im[b]


def radiate_kernel(coef_ref, points_ref, observer_ref, acc_ref, amp_a, amp_b, cos_a, cos_b, sin_a, sin_b):
    pairs = coef_ref.shape[0]
    observers = observer_ref[...]
    acc_ref[...] = jnp.zeros_like(acc_ref)

    def prepare(pair):
        both = coef_ref[pair]
        half = both.shape[1] // 2
        first = lax.broadcasted_iota(jnp.int32, both.shape, 1) < half
        high, low = split_hi_lo(both)
        left_a = jnp.where(first, high, pltpu.roll(low, half, 1)).astype(jnp.bfloat16)
        left_b = jnp.where(first, pltpu.roll(high, half, 1), low).astype(jnp.bfloat16)
        return jnp.concatenate([left_a, left_a], axis=1), jnp.concatenate([left_b, left_b], axis=1)

    def points_at(group):
        return points_ref[pl.ds(pl.multiple_of(group * GROUP, GROUP), GROUP), :]

    left, _ = prepare(0)
    amplitude(left, geometry(points_at(0), observers, cos_a, sin_a), amp_a)

    @pl.loop(0, pairs)
    def _(pair):
        _, left_b = prepare(pair)
        amplitude(left_b, geometry(points_at(2 * pair + 1), observers, cos_b, sin_b), amp_b)
        accumulate(amp_a, cos_a, sin_a, acc_ref)
        after = jnp.minimum(pair + 1, pairs - 1)
        left_a, _ = prepare(after)
        amplitude(left_a, geometry(points_at(2 * after), observers, cos_a, sin_a), amp_a)
        accumulate(amp_b, cos_b, sin_b, acc_ref)


def radiate_all(spectra, points, observers):
    orders = spectra.shape[2] // 2
    panels = spectra.shape[1]
    wavenum = KAPPA * jnp.arange(1, orders + 1, dtype=jnp.float32)
    turned = jnp.concatenate(
        [-wavenum * spectra[:, :, orders:], wavenum * spectra[:, :, :orders]], axis=2
    )
    slots = jnp.concatenate(
        [spectra[1:4], turned[1:4], turned[0:1], jnp.zeros_like(turned[0:1])], axis=0
    )
    pairs = panels // (2 * GROUP)
    coefs = slots.reshape(SLOT, pairs, 2, GROUP, 2 * orders).transpose(1, 2, 0, 3, 4)
    coefs = coefs.reshape(pairs, 2 * SLOT * GROUP, 2 * orders).transpose(0, 2, 1)
    count = observers.shape[1]
    wave = pltpu.VMEM((8, GROUP, count), jnp.float32)
    amp = pltpu.VMEM((GROUP * 2 * orders, count), jnp.float32)
    return pl.pallas_call(
        radiate_kernel,
        out_shape=jax.ShapeDtypeStruct((2 * orders, count), jnp.float32),
        in_specs=[pl.BlockSpec(memory_space=pltpu.VMEM)] * 3,
        out_specs=pl.BlockSpec(memory_space=pltpu.VMEM),
        scratch_shapes=[amp, amp, wave, wave, wave, wave],
        name="radiate",
    )(coefs, points.T, observers)


def total_kernel(axis, source_ref, sum_ref, held_ref, send_sem, recv_sem, local_sem):
    swap_kernel(axis, True, source_ref, held_ref, send_sem, recv_sem, local_sem)
    total = held_ref[0]
    for peer in range(1, held_ref.shape[0]):
        total = total + held_ref[peer]
    sum_ref[...] = total


def swap_kernel(axis, spread, source_ref, out_ref, send_sem, recv_sem, local_sem):
    peers = out_ref.shape[0]
    me = lax.axis_index(axis)
    barrier = pltpu.get_barrier_semaphore()
    for shift in range(1, peers):
        pl.semaphore_signal(
            barrier,
            inc=1,
            device_id={axis: lax.rem(me + shift, peers)},
            device_id_type=pl.DeviceIdType.MESH,
        )
    own = pltpu.make_async_copy(source_ref.at[me] if spread else source_ref, out_ref.at[me], local_sem)
    own.start()
    pl.semaphore_wait(barrier, peers - 1)
    copies = []
    for shift in range(1, peers):
        target = lax.rem(me + shift, peers)
        copy = pltpu.make_async_remote_copy(
            src_ref=source_ref.at[target] if spread else source_ref,
            dst_ref=out_ref.at[me],
            send_sem=send_sem.at[shift],
            recv_sem=recv_sem.at[shift],
            device_id={axis: target},
            device_id_type=pl.DeviceIdType.MESH,
        )
        copy.start()
        copies.append(copy)
    own.wait()
    for copy in copies:
        copy.wait()


def swap(array, axis, spread, number):
    peers = lax.axis_size(axis)
    shape = array.shape if spread else (peers,) + array.shape
    return pl.pallas_call(
        functools.partial(swap_kernel, axis, spread),
        out_shape=jax.ShapeDtypeStruct(shape, array.dtype),
        in_specs=[pl.BlockSpec(memory_space=pltpu.VMEM)],
        out_specs=pl.BlockSpec(memory_space=pltpu.VMEM),
        scratch_shapes=[
            pltpu.SemaphoreType.DMA((peers,)),
            pltpu.SemaphoreType.DMA((peers,)),
            pltpu.SemaphoreType.DMA,
        ],
        compiler_params=pltpu.CompilerParams(collective_id=number, has_side_effects=True),
        name=f"swap{number}",
    )(array)


def swap_total(array, axis, number):
    peers = lax.axis_size(axis)
    return pl.pallas_call(
        functools.partial(total_kernel, axis),
        out_shape=jax.ShapeDtypeStruct(array.shape[1:], array.dtype),
        in_specs=[pl.BlockSpec(memory_space=pltpu.VMEM)],
        out_specs=pl.BlockSpec(memory_space=pltpu.VMEM),
        scratch_shapes=[
            pltpu.VMEM(array.shape, array.dtype),
            pltpu.SemaphoreType.DMA((peers,)),
            pltpu.SemaphoreType.DMA((peers,)),
            pltpu.SemaphoreType.DMA,
        ],
        compiler_params=pltpu.CompilerParams(collective_id=number, has_side_effects=True),
        name=f"swap{number}",
    )(array)


def hot(condition):
    return condition.astype(jnp.bfloat16)


def body(
    flow_blocks,
    interp_weights,
    donor_owner,
    donor_block,
    panel_normals,
    panel_points,
    observer_points,
):
    peer_count = lax.axis_size("panel")
    me = lax.axis_index("panel")
    tile_count, tile_width, stencil = interp_weights.shape
    held_count, cell_count, history = flow_blocks.shape
    slot_count = stencil // cell_count
    row_count = tile_count * slot_count
    capacity = max(2, (3 * row_count + 2 * peer_count - 1) // (2 * peer_count))
    owner_of = donor_owner[:, 0]
    wanted = swap(jnp.stack([owner_of, donor_block]), "panel", False, 1)
    rows = jnp.arange(row_count, dtype=jnp.int32)
    upto = hot(rows[:, None] <= rows[None, :])
    asked = wanted[:, 0] == me
    rank = jnp.dot(hot(asked), upto, preferred_element_type=jnp.float32).astype(jnp.int32) - 1
    place = jnp.arange(capacity, dtype=jnp.int32)
    chosen = hot(asked[:, None, :] & (rank[:, None, :] == place[None, :, None]))
    named = hot(wanted[:, 1][:, :, None] == jnp.arange(held_count, dtype=jnp.int32)[None, None, :])
    select = jnp.einsum("qsr,qrb->qsb", chosen, named, preferred_element_type=jnp.float32)
    select = select.astype(jnp.bfloat16).reshape(peer_count * capacity, held_count)
    flat = flow_blocks.reshape(held_count, cell_count * history)
    found = jnp.dot(select, flat, preferred_element_type=jnp.float32).astype(jnp.bfloat16)
    arrived = swap(found.reshape(peer_count, capacity, -1), "panel", True, 2)
    arrived = arrived.reshape(peer_count * capacity, -1)
    matches = owner_of[:, None] == jnp.arange(peer_count, dtype=jnp.int32)[None, :]
    counts = jnp.dot(upto.T, hot(matches), preferred_element_type=jnp.float32)
    own_rank = jnp.sum(jnp.where(matches, counts, 0.0), axis=1).astype(jnp.int32) - 1
    target = jnp.repeat(owner_of * capacity + own_rank, cell_count).reshape(tile_count, stencil)
    lines = jnp.arange(peer_count * capacity, dtype=jnp.int32)
    cell_of = jnp.arange(stencil, dtype=jnp.int32) % cell_count
    values = 0.0
    for cell in range(cell_count):
        moved = hot((target[:, :, None] == lines) & (cell_of == cell)[None, :, None])
        weights = jnp.einsum("tpj,tjk->tpk", interp_weights, moved, preferred_element_type=jnp.float32)
        values = values + jnp.einsum(
            "tpk,kv->tpv",
            weights.astype(jnp.bfloat16),
            arrived[:, cell * history : (cell + 1) * history],
            preferred_element_type=jnp.float32,
        )
    values = values.reshape(tile_count * tile_width, history)
    transform = fourier_table(NT, HARM)
    spectra = spectra_of(values, panel_normals, transform, NT)
    series_count, panels, lanes = spectra.shape
    padded = jnp.pad(panel_points, ((0, 5), (0, 0))).reshape(-1, lanes)
    packed = jnp.concatenate([spectra.reshape(-1, lanes), padded], axis=0)
    group = swap(packed, "obs", False, 3)
    cut = series_count * panels
    all_spectra = group[:, :cut].reshape(-1, series_count, panels, lanes).transpose(1, 0, 2, 3)
    all_spectra = all_spectra.reshape(series_count, -1, lanes)
    all_points = group[:, cut:].reshape(-1, 8, panels)[:, :3].transpose(1, 0, 2).reshape(3, -1)
    partial_sum = radiate_all(all_spectra, all_points, observer_points)
    terms = partial_sum.reshape(peer_count, -1, partial_sum.shape[1])
    return swap_total(terms, "panel", 4)


def solution(mesh):
    return jax.shard_map(
        body,
        mesh=mesh,
        in_specs=(
            P("panel", None, None),
            P(("panel", "obs"), None, None),
            P(("panel", "obs"), None),
            P(("panel", "obs")),
            P(None, ("panel", "obs")),
            P(None, ("panel", "obs")),
            P(None, "obs"),
        ),
        out_specs=P("panel", "obs"),
        check_vma=False,
    )
```

profile of v0, /device:TPU:0, one launch (start us, length us, event | category | flops | bytes accessed | tf_op | source)
XLA Modules:
  0.0 141.0 jit_solution(2554510666385570416)
XLA Ops:
  0.0 0.9 fusion.2
  0.9 0.7 add_add_fusion
  1.6 0.5 fusion.69
  2.2 0.5 fusion.68
  2.7 0.5 fusion.67
  3.2 1.2 pad_add_fusion.source_ref
  4.5 9.6 %swap1.1 = s32[8,2,128]{2,1,0:T(2,128)} custom-call(s32[2,128]{1,0:T(2,128)} %pad_add_fusion.source_ref), custom_call_target="tpu_custom_call" | custom-call | tf_op jit(solution)/shard_map/swap1/pallas_call | solution.py:230
  14.1 0.7 slice_compare_fusion
  14.8 0.7 slice.52
  15.7 0.3 convolution_convert_fusion.4
  16.2 1.2 cosine_multiply_fusion
  17.4 1.5 %copy.22 = bf16[16,8,4,1280]{3,1,2,0:T(8,128)(2,1)S(1)} copy(bf16[16,8,4,1280]{3,2,1,0:T(4,128)(2,1)} %bitcast.93) | data formatting | bytes 2621440
  18.9 1.9 %convolution_convert_fusion = bf16[192,5120]{1,0:T(8,128)(2,1)} fusion(bf16[192,128]{1,0:T(8,128)(2,1)S(1)} %bitcast.99, bf16[128,5120]{1,0:T(8,128)(2,1)S(1)} %bitcast.87), kind=kOutput, calls=%fused_computation | convolution fusion | flops 252641280 | bytes 3325952 | tf_op jit(solution)/shard_map/dot_general | solution.py:295
  20.8 37.6 %swap2.1 = bf16[8,24,5120]{2,1,0:T(8,128)(2,1)} custom-call(bf16[8,24,5120]{2,1,0:T(8,128)(2,1)} %bitcast.82), custom_call_target="tpu_custom_call" | custom-call | tf_op jit(solution)/shard_map/swap2/pallas_call | solution.py:230
  58.4 1.7 %fusion = f32[128,1280]{1,0:T(8,128)S(1)} fusion(bf16[192,5120]{1,0:T(8,128)(2,1)} %bitcast.83, s32[512]{0:T(512)S(1)} %eq.180, pred[512]{0:T(512)(128)(4,1)S(1)} %fusion.70, bf16[1,128,512]{2,1,0:T(8,128)(2,1)S(1)} %copy-done), kind=kOutput, calls=%fused_computation.10 | convolution fusion | flops 88301568 | bytes 1280512 | tf_op jit(solution)/shard_map/tpk,kv->tpv/dot_general | solution.py:308
  60.1 1.6 %convolution_add_fusion.2 = f32[128,1280]{1,0:T(8,128)S(1)} fusion(f32[128,1280]{1,0:T(8,128)S(1)} %fusion, bf16[192,5120]{1,0:T(8,128)(2,1)} %bitcast.84, s32[512]{0:T(512)S(1)} %eq.180, pred[512]{0:T(512)(128)(4,1)} %fusion.69, bf16[1,128,512]{2,1,0:T(8,128)(2,1)S(1)} %copy-done), kind=kOutput, calls=%fused_computation.3 | convolution fusion | flops 88465408 | bytes 1935872 | tf_op jit(solution)/shard_map/tpk,kv->tpv/dot_general | solution.py:308
  61.7 1.2 convolution_add_fusion.1
  62.9 1.2 convolution_add_fusion
  65.3 0.7 fusion.4
  66.0 0.7 select_maximum_fusion.source_ref
  66.7 15.4 %swap3.1 = f32[4,520,128]{2,1,0:T(8,128)} custom-call(f32[520,128]{1,0:T(8,128)} %select_maximum_fusion.source_ref), custom_call_target="tpu_custom_call" | custom-call | tf_op jit(solution)/shard_map/swap3/pallas_call | solution.py:230
  82.1 0.8 slice_bitcast_fusion.1
  82.9 0.4 slice-done
  83.4 0.9 copy.18
  84.4 0.4 slice_multiply_fusion.1
  84.9 0.3 fusion.3
  85.1 0.3 maximum_bitcast_fusion
  85.4 0.3 copy.16
  85.7 1.9 %copy.17 = f32[32,128,128]{1,2,0:T(8,128)} copy(f32[32,128,128]{2,1,0:T(8,128)S(1)} %bitcast.81) | data formatting | bytes 4194304 | tf_op jit(solution)/shard_map/reshape | solution.py:173
  87.5 31.8 %radiate.1 = f32[128,256]{1,0:T(8,128)} custom-call(f32[32,128,128]{2,1,0:T(8,128)} %bitcast.80, f32[512,3]{1,0:T(8,128)} %bitcast.96, f32[3,256]{1,0:T(4,128)} %observer_ref.1), custom_call_target="tpu_custom_call" | custom-call | tf_op jit(solution)/shard_map/radiate/pallas_call | solution.py:177
  119.4 20.3 %swap4.1 = f32[16,256]{1,0:T(8,128)} custom-call(f32[8,16,256]{2,1,0:T(8,128)} %bitcast.98), custom_call_target="tpu_custom_call" | custom-call | tf_op jit(solution)/shard_map/swap4/pallas_call | solution.py:247
  139.7 1.3 copy.29
  (31 shorter events, 1.8 us)
Async XLA Ops:
  0.0 58.4 %copy-start = (bf16[1,128,512]{2,1,0:T(8,128)(2,1)S(1)}, bf16[1,128,512]{2,1,0:T(8,128)(2,1)}, u32[]{:S(2)}) copy-start(bf16[1,128,512]{2,1,0:T(8,128)(2,1)} %param.8) | copy-start | bytes 393220
  58.4 3.4 %copy-start.1 = (bf16[8,24,5120]{2,1,0:T(8,128)(2,1)S(1)}, bf16[8,24,5120]{2,1,0:T(8,128)(2,1)}, u32[]{:S(2)}) copy-start(bf16[8,24,5120]{2,1,0:T(8,128)(2,1)} %swap2.1) | copy-start | bytes 5898244
  64.1 0.7 copy-start.3
  64.4 0.9 copy-start.2
  64.6 1.4 copy-start.4
  82.1 1.2 slice-start
where the time goes:
time: 142 us; the launch traced here: 141 us
  Pallas kernels  115 us (81%)
  matrix products  9.58 us (7%)
  local copies, waits for them, and re-layouts  8.96 us (6%)
  other arithmetic  7.43 us (5%)
    pallas_call x3, Pallas kernels, swap(): pl.pallas_call(functools.partial(swap_kernel, axis, spread), out_shape=ja...  62.6 us
    pallas_call x1, Pallas kernels, radiate_all(): pl.pallas_call(radiate_kernel, out_shape=jax.ShapeDtypeStruct((2 * orders...  31.8 us
    pallas_call x1, Pallas kernels, swap_total(): pl.pallas_call(functools.partial(total_kernel, axis), out_shape=jax.Shape...  20.3 us
    dot_general x4, matrix products, body(): jnp.einsum('tpk,kv->tpv', weights.astype(jnp.bfloat16), arrived[:, cell *...  5.68 us
    unnamed x15, local copies, waits for them, and re-layouts  3.27 us

commit v1 on v0

v1 whole, which is shorter than its diff:
```python
import functools
import math

import jax
import jax.numpy as jnp
import numpy as np
from jax import lax
from jax.experimental import pallas as pl
from jax.experimental.pallas import tpu as pltpu
from jax.sharding import PartitionSpec as P

NV = 5
NT = 256
HARM = 64
SERIES = 4
GROUP = 8
SLOT = 8
KAPPA = 0.5
MESH = pl.DeviceIdType.MESH


def fourier_rows(samples, orders):
    wrapped = np.arange(1, orders + 1)[:, None] * np.arange(samples)[None, :] % samples
    angles = wrapped * (2.0 * np.pi / samples)
    factor = 2.0 / samples
    return np.concatenate([factor * np.cos(angles), -factor * np.sin(angles)], axis=0).astype(np.float32)


def flip(index, bits, width):
    out = index
    bit = 1
    while bit < width:
        mine = lax.rem(index // bit, 2) if not isinstance(index, int) else (index // bit) % 2
        theirs = lax.rem(bits // bit, 2) if not isinstance(bits, int) else (bits // bit) % 2
        if not isinstance(bits, int) or theirs:
            out = out + bit * theirs * (1 - 2 * mine)
        bit *= 2
    return out


def hot(condition):
    return jnp.where(condition, 1.0, 0.0).astype(jnp.bfloat16)


def across(left, right):
    return lax.dot_general(left, right, (((1,), (1,)), ((), ())), preferred_element_type=jnp.float32)


def series_kernel(
    share,
    flow_ref,
    weight_ref,
    owner_ref,
    block_ref,
    normal_ref,
    observer_ref,
    series_ref,
    observers_ref,
    slices,
    flows,
    weights,
    facts,
    onehot,
    outgoing,
    flow_send,
    flow_recv,
    weight_send,
    weight_recv,
    fact_send,
    fact_recv,
    view_send,
    view_recv,
    series_send,
    series_recv,
):
    owners = flows.shape[0]
    held = flow_ref.shape[1]
    cells = flow_ref.shape[0]
    spread = observers_ref.shape[0]
    members = share * spread
    samples = NT // members
    width = NV * samples
    slots = weight_ref.shape[1] // cells
    me_panel = lax.axis_index("panel")
    me_obs = lax.axis_index("obs")
    sub = lax.rem(me_panel, share)
    base = me_panel - sub
    mine = me_obs * share + sub

    def member(distance):
        return {
            "panel": base + flip(sub, distance // spread, share),
            "obs": flip(me_obs, distance % spread if isinstance(distance, int) else lax.rem(distance, spread), spread),
        }

    barrier = pltpu.get_barrier_semaphore()
    for distance in range(1, members):
        pl.semaphore_signal(barrier, inc=1, device_id=member(distance), device_id_type=MESH)

    def greet(shift, carry):
        target = lax.rem(me_panel + shift, owners)
        pl.semaphore_signal(barrier, inc=1, device_id={"panel": target}, device_id_type=MESH)
        return carry

    lax.fori_loop(1, owners, greet, 0)

    quarter = share * samples
    rows = lax.broadcasted_iota(jnp.int32, (quarter, NT), 0)
    columns = lax.broadcasted_iota(jnp.int32, (quarter, NT), 1)
    pick = hot(columns == rows + me_obs * quarter)
    for cell in range(cells):
        for var in range(NV):
            piece = across(pick, flow_ref[cell, :, var * NT : (var + 1) * NT]).astype(jnp.bfloat16)
            for part in range(share):
                row = cell * width + var * samples
                slices[part, row : row + samples, :] = piece[part * samples : (part + 1) * samples, :]
    facts[0] = jnp.zeros(facts.shape[1:], jnp.float32)
    facts[0, 0:1, :] = owner_ref[...].astype(jnp.float32)
    facts[0, 1:2, :] = block_ref[...].astype(jnp.float32)
    facts[0, 2:5, :] = normal_ref[...]
    place = lax.broadcasted_iota(jnp.int32, (slots * cells, slots * cells), 0)
    goal = lax.broadcasted_iota(jnp.int32, (slots * cells, slots * cells), 1)
    turn = hot(lax.rem(place, cells) * slots + place // cells == goal)
    weights[0] = jnp.dot(weight_ref[...], turn, preferred_element_type=jnp.float32).astype(jnp.bfloat16)
    observers_ref[me_obs] = observer_ref[...]

    pl.semaphore_wait(barrier, members - 1 + owners - 1)

    def flow_copy(shift):
        target = lax.rem(me_panel + shift, owners)
        return pltpu.make_async_remote_copy(
            src_ref=slices.at[lax.rem(target, share)],
            dst_ref=flows.at[me_panel],
            send_sem=flow_send.at[shift],
            recv_sem=flow_recv.at[shift],
            device_id={"panel": target},
            device_id_type=MESH,
        )

    def push(shift, carry):
        flow_copy(shift).start()
        return carry

    lax.fori_loop(1, owners, push, 0)

    def relay(buffer, send_sem, recv_sem, held_slot, bit):
        return pltpu.make_async_remote_copy(
            src_ref=buffer.at[held_slot],
            dst_ref=buffer.at[held_slot + bit],
            send_sem=send_sem.at[held_slot + bit],
            recv_sem=recv_sem.at[held_slot + bit],
            device_id=member(bit),
            device_id_type=MESH,
        )

    bits = []
    bit = members // 2
    while bit >= 1:
        bits.append(bit)
        bit //= 2
    copies = {}

    def forward(slot):
        lowest = members if slot == 0 else slot & -slot
        for bit in bits:
            if bit < lowest:
                for kind, (buffer, send_sem, recv_sem) in enumerate(
                    ((facts, fact_send, fact_recv), (weights, weight_send, weight_recv))
                ):
                    copy = relay(buffer, send_sem, recv_sem, slot, bit)
                    copy.start()
                    copies[kind, slot + bit] = copy

    forward(0)

    def view_copy(shift):
        return pltpu.make_async_remote_copy(
            src_ref=observer_ref,
            dst_ref=observers_ref.at[me_obs],
            send_sem=view_send.at[shift],
            recv_sem=view_recv.at[shift],
            device_id={"obs": lax.rem(me_obs + shift, spread)},
            device_id_type=MESH,
        )

    views = [view_copy(shift) for shift in range(1, spread)]
    for view in views:
        view.start()
    flows[me_panel] = slices[sub]
    order = sorted(range(1, members), key=lambda slot: (bin(slot).count("1"), -slot))
    for slot in order:
        copies[0, slot].wait_recv()
        copies[1, slot].wait_recv()
        forward(slot)

    names = lax.broadcasted_iota(jnp.int32, (held, slots), 0).astype(jnp.float32)

    def mark(slot, side):
        owner_row = facts[slot, 0:1, :]
        block_row = facts[slot, 1:2, :]

        def mark_owner(owner, inner):
            row = jnp.where(owner_row == owner.astype(jnp.float32), block_row, -1.0)
            onehot[side, pl.ds(pl.multiple_of(owner * held, held), held), :] = hot(names == row)
            return inner

        lax.fori_loop(0, owners, mark_owner, 0)

    def drain(shift, carry):
        flow_copy(shift).wait()
        return carry

    lax.fori_loop(1, owners, drain, 0)

    chunk = min(owners, 8)

    def gathered(low, high):
        mark(low, 0)
        mark(high, 1)

        def partial_of(start):
            left = jnp.concatenate([flows[start + i] for i in range(chunk)], axis=1)
            row = pl.ds(pl.multiple_of(start * held, held), chunk * held)
            right = jnp.concatenate([onehot[0, row, :], onehot[1, row, :]], axis=1)
            return jnp.dot(left, right, preferred_element_type=jnp.float32)

        total = partial_of(0)
        if owners > chunk:
            total = lax.fori_loop(1, owners // chunk, lambda i, run: run + partial_of(i * chunk), total)
        return total.astype(jnp.bfloat16)

    def series_of(slot, donors):
        left = jnp.concatenate([donors[cell * width : (cell + 1) * width, :] for cell in range(cells)], axis=1)
        values = across(left, weights[slot])
        field = [values[var * samples : (var + 1) * samples, :] for var in range(NV)]
        normal = [facts[slot, 2 + i : 3 + i, :] for i in range(3)]
        flow = field[1] * normal[0] + field[2] * normal[1] + field[3] * normal[2]
        mass = (1.0 + field[0]) * flow
        return [mass] + [field[4] * normal[i] + mass * field[1 + i] for i in range(3)]

    span = pl.ds(pl.multiple_of(mine * samples, samples), samples)

    def series_copy(slot):
        return pltpu.make_async_remote_copy(
            src_ref=outgoing.at[slot],
            dst_ref=series_ref.at[:, span, :],
            send_sem=series_send.at[slot],
            recv_sem=series_recv.at[slot],
            device_id=member(slot),
            device_id_type=MESH,
        )

    def finish(slot, donors):
        for kind, term in enumerate(series_of(slot, donors)):
            outgoing[slot, kind] = term
        series_copy(slot).start()

    first = gathered(0, 1)
    for kind, term in enumerate(series_of(0, first[:, :slots])):
        series_ref[kind, span, :] = term
    finish(1, first[:, slots:])

    def pair(step, carry):
        both = gathered(2 * step, 2 * step + 1)
        finish(2 * step, both[:, :slots])
        finish(2 * step + 1, both[:, slots:])
        return carry

    lax.fori_loop(1, members // 2, pair, 0)

    for slot in range(1, members):
        copies[0, slot].wait_send()
        copies[1, slot].wait_send()
    for view in views:
        view.wait()

    def settle(slot, carry):
        series_copy(slot).wait()
        return carry

    lax.fori_loop(1, members, settle, 0)


def series_all(flow, weight, owner, block, normals, observers):
    owners = lax.axis_size("panel")
    spread = lax.axis_size("obs")
    share = max(1, min(owners, 16 // spread))
    members = share * spread
    cells, held, history = flow.shape
    panels = normals.shape[1]
    samples = NT // members
    width = NV * samples
    bf16, f32 = jnp.bfloat16, jnp.float32
    vmem = pl.BlockSpec(memory_space=pltpu.VMEM)
    dma = pltpu.SemaphoreType.DMA
    return pl.pallas_call(
        functools.partial(series_kernel, share),
        out_shape=(
            jax.ShapeDtypeStruct((SERIES, NT, panels), f32),
            jax.ShapeDtypeStruct((spread,) + observers.shape, f32),
        ),
        in_specs=[vmem] * 6,
        out_specs=(vmem, vmem),
        scratch_shapes=[
            pltpu.VMEM((share, cells * width, held), bf16),
            pltpu.VMEM((owners, cells * width, held), bf16),
            pltpu.VMEM((members,) + weight.shape, bf16),
            pltpu.VMEM((members, 8, panels), f32),
            pltpu.VMEM((2, owners * held, weight.shape[1] // cells), bf16),
            pltpu.VMEM((members, SERIES, samples, panels), f32),
            dma((owners,)),
            dma((owners,)),
            dma((members,)),
            dma((members,)),
            dma((members,)),
            dma((members,)),
            dma((spread,)),
            dma((spread,)),
            dma((members,)),
            dma((members,)),
        ],
        compiler_params=pltpu.CompilerParams(collective_id=1, has_side_effects=True, vmem_limit_bytes=60 * 1024 * 1024),
        name="series",
    )(flow, weight, owner, block, normals, observers)


def sin_cos(angle):
    turns = jnp.floor(angle * (2.0 / math.pi) + 0.5)
    reduced = angle - turns * 1.5703125
    reduced = reduced - turns * 4.837512969970703125e-4
    reduced = reduced - turns * 7.54978995489188216e-8
    square = reduced * reduced
    sine = ((-1.9515295891e-4 * square + 8.3321608736e-3) * square - 1.6666654611e-1) * square * reduced + reduced
    cosine = ((2.443315711809948e-5 * square - 1.388731625493765e-3) * square + 4.166664568298827e-2) * square * square - 0.5 * square + 1.0
    quadrant = turns.astype(jnp.int32)
    swap = (quadrant & 1) == 1
    out_sin = jnp.where(swap, cosine, sine)
    out_cos = jnp.where(swap, sine, cosine)
    out_sin = jnp.where((quadrant & 2) == 2, -out_sin, out_sin)
    out_cos = jnp.where(((quadrant + 1) & 2) == 2, -out_cos, out_cos)
    return out_sin, out_cos


def split_hi_lo(array):
    high = array.astype(jnp.bfloat16).astype(jnp.float32)
    return high, array - high


def geometry(points, observers, cos_ref, sin_ref):
    offsets = [observers[i : i + 1, :] - points[:, i : i + 1] for i in range(3)]
    squared = offsets[0] * offsets[0] + offsets[1] * offsets[1] + offsets[2] * offsets[2]
    distance = jnp.sqrt(squared)
    inverse = 1.0 / distance
    weight = inverse * (1.0 / (4.0 * math.pi))
    far = [offset * (inverse * weight) for offset in offsets]
    near = [term * inverse for term in far]
    slots = near + far + [weight, jnp.zeros_like(weight)]
    high, low = split_hi_lo(jnp.concatenate(slots, axis=0))
    right = jnp.concatenate([high, high, low, low], axis=0).astype(jnp.bfloat16)
    sine, cosine = sin_cos(KAPPA * distance)
    twice = 2.0 * cosine
    past_cos, past_sin = jnp.ones_like(cosine), jnp.zeros_like(sine)
    for order in range(8):
        cos_ref[order] = cosine
        sin_ref[order] = sine
        cosine, past_cos = twice * cosine - past_cos, cosine
        sine, past_sin = twice * sine - past_sin, sine
    return right


def amplitude(left, right, out_ref):
    lanes = lax.broadcasted_iota(jnp.int32, (1, left.shape[1]), 1) % GROUP
    masked = [left * (lanes == y).astype(jnp.float32).astype(jnp.bfloat16) for y in range(GROUP)]
    stacked = jnp.concatenate(masked, axis=0)
    out_ref[...] = jnp.dot(stacked, right, preferred_element_type=jnp.float32)


def accumulate(amp_ref, cos_ref, sin_ref, acc_ref):
    rows, observers = acc_ref.shape
    orders = rows // 2
    blocks = orders // 8
    for half in range(observers // 128):
        lane = pl.ds(half * 128, 128)
        acc_re = [acc_ref[pl.ds(8 * b, 8), lane] for b in range(blocks)]
        acc_im = [acc_ref[pl.ds(orders + 8 * b, 8), lane] for b in range(blocks)]
        for y in range(GROUP):
            cosine = cos_ref[:, y, lane]
            sine = sin_ref[:, y, lane]
            step_cos = cos_ref[7, pl.ds(y, 1), lane]
            step_sin = sin_ref[7, pl.ds(y, 1), lane]
            twice = 2.0 * step_cos
            past_cos = past_sin = None
            for b in range(blocks):
                amp_re = amp_ref[pl.ds(y * rows + 8 * b, 8), lane]
                amp_im = amp_ref[pl.ds(y * rows + orders + 8 * b, 8), lane]
                acc_re[b] = acc_re[b] + (amp_re * cosine + amp_im * sine)
                acc_im[b] = acc_im[b] + (amp_im * cosine - amp_re * sine)
                if b == 0:
                    next_cos = cosine * step_cos - sine * step_sin
                    next_sin = sine * step_cos + cosine * step_sin
                else:
                    next_cos = twice * cosine - past_cos
                    next_sin = twice * sine - past_sin
                past_cos, past_sin, cosine, sine = cosine, sine, next_cos, next_sin
        for b in range(blocks):
            acc_ref[pl.ds(8 * b, 8), lane] = acc_re[b]
            acc_ref[pl.ds(orders + 8 * b, 8), lane] = acc_im[b]


def radiate_kernel(
    series_ref,
    table_ref,
    point_ref,
    observers_ref,
    out_ref,
    terms,
    points,
    lefts,
    acc_ref,
    amp_a,
    amp_b,
    cos_a,
    cos_b,
    sin_a,
    sin_b,
    outgoing,
    arrived,
    send_sem,
    recv_sem,
):
    owners = lax.axis_size("panel")
    spread = lax.axis_size("obs")
    me_panel = lax.axis_index("panel")
    me_obs = lax.axis_index("obs")
    orders = acc_ref.shape[0] // 2
    panels = point_ref.shape[1]
    groups = panels // GROUP
    rows = out_ref.shape[0]
    barrier = pltpu.get_barrier_semaphore()
    for turn in range(spread):

        def greet(shift, carry):
            pl.semaphore_signal(
                barrier,
                inc=1,
                device_id={"panel": lax.rem(me_panel + shift, owners), "obs": lax.rem(me_obs + turn, spread)},
                device_id_type=MESH,
            )
            return carry

        lax.fori_loop(1 if turn == 0 else 0, owners, greet, 0)

    points[...] = jnp.zeros_like(points)
    points[0:3, :] = point_ref[...]
    points[...] = jnp.transpose(points[...])
    wavenum = KAPPA * (1 + lax.broadcasted_iota(jnp.int32, (orders, panels), 0)).astype(jnp.float32)
    for kind in range(SERIES):
        near = jnp.dot(
            table_ref[...], series_ref[kind], preferred_element_type=jnp.float32, precision=lax.Precision.HIGHEST
        )
        far = jnp.concatenate([-wavenum * near[orders:], wavenum * near[:orders]], axis=0)
        if kind == 0:
            terms[6] = far
        else:
            terms[kind - 1] = near
            terms[kind + 2] = far
    lane = lax.broadcasted_iota(jnp.int32, (2 * orders, panels), 1)

    @pl.loop(0, groups)
    def _(group):
        both = jnp.zeros((2 * orders, panels), jnp.float32)
        for slot in range(SLOT - 1):
            moved = pltpu.roll(terms[slot], lax.rem(panels + (slot - group) * GROUP, panels), 1)
            both = jnp.where(lane // GROUP == slot, moved, both)
        high, low = split_hi_lo(both)
        lefts[group] = jnp.where(lane < SLOT * GROUP, high, pltpu.roll(low, SLOT * GROUP, 1)).astype(jnp.bfloat16)

    pl.semaphore_wait(barrier, owners * spread - 1)

    def left_of(group):
        left = lefts[group]
        return jnp.concatenate([left, left], axis=1)

    def points_at(group):
        return points[pl.ds(pl.multiple_of(group * GROUP, GROUP), GROUP), :]

    def term_copy(step, shift):
        slot = lax.rem(step + 1, spread) * owners + shift
        target = lax.rem(me_panel + shift, owners)
        return pltpu.make_async_remote_copy(
            src_ref=outgoing.at[step, target],
            dst_ref=arrived.at[slot],
            send_sem=send_sem.at[slot],
            recv_sem=recv_sem.at[slot],
            device_id={"panel": target, "obs": lax.rem(me_obs + step + 1, spread)},
            device_id_type=MESH,
        )

    @pl.loop(0, spread)
    def _(step):
        observers = observers_ref[lax.rem(me_obs + step + 1, spread)]
        acc_ref[...] = jnp.zeros_like(acc_ref)
        amplitude(left_of(0), geometry(points_at(0), observers, cos_a, sin_a), amp_a)

        @pl.loop(0, groups // 2)
        def _(pair):
            amplitude(left_of(2 * pair + 1), geometry(points_at(2 * pair + 1), observers, cos_b, sin_b), amp_b)
            accumulate(amp_a, cos_a, sin_a, acc_ref)
            after = jnp.minimum(pair + 1, groups // 2 - 1)
            amplitude(left_of(2 * after), geometry(points_at(2 * after), observers, cos_a, sin_a), amp_a)
            accumulate(amp_b, cos_b, sin_b, acc_ref)

        for owner in range(owners):
            outgoing[step, owner] = acc_ref[owner * rows : (owner + 1) * rows, :]

        @pl.when(step < spread - 1)
        def _():
            term_copy(step, 0).start()

        def push(shift, carry):
            term_copy(step, shift).start()
            return carry

        lax.fori_loop(1, owners, push, 0)

    arrived[0] = outgoing[spread - 1, me_panel]
    for step in range(spread):

        def settle(shift, carry):
            term_copy(step, shift).wait()
            return carry

        lax.fori_loop(1 if step == spread - 1 else 0, owners, settle, 0)

    def add(slot, total):
        return total + arrived[slot]

    out_ref[...] = lax.fori_loop(1, owners * spread, add, arrived[0])


def radiate_all(series, points, observers):
    owners = lax.axis_size("panel")
    spread = lax.axis_size("obs")
    panels = points.shape[1]
    count = observers.shape[2]
    rows = 2 * HARM // owners
    f32 = jnp.float32
    wave = pltpu.VMEM((8, GROUP, count), f32)
    amp = pltpu.VMEM((GROUP * 2 * HARM, count), f32)
    return pl.pallas_call(
        radiate_kernel,
        out_shape=jax.ShapeDtypeStruct((rows, count), f32),
        in_specs=[pl.BlockSpec(memory_space=pltpu.VMEM)] * 4,
        out_specs=pl.BlockSpec(memory_space=pltpu.VMEM),
        scratch_shapes=[
            pltpu.VMEM((SLOT - 1, 2 * HARM, panels), f32),
            pltpu.VMEM((panels, panels), f32),
            pltpu.VMEM((panels // GROUP, 2 * HARM, panels), jnp.bfloat16),
            pltpu.VMEM((2 * HARM, count), f32),
            amp,
            amp,
            wave,
            wave,
            wave,
            wave,
            pltpu.VMEM((spread, owners, rows, count), f32),
            pltpu.VMEM((spread * owners, rows, count), f32),
            pltpu.SemaphoreType.DMA((spread * owners,)),
            pltpu.SemaphoreType.DMA((spread * owners,)),
        ],
        compiler_params=pltpu.CompilerParams(collective_id=2, has_side_effects=True, vmem_limit_bytes=60 * 1024 * 1024),
        name="radiate",
    )(series, jnp.asarray(fourier_rows(NT, HARM)), points, observers)


def body(
    flow_blocks,
    interp_weights,
    donor_owner,
    donor_block,
    panel_normals,
    panel_points,
    observer_points,
):
    tiles, width, stencil = interp_weights.shape
    series, observers = series_all(
        flow_blocks.transpose(1, 0, 2),
        interp_weights.reshape(tiles * width, stencil),
        donor_owner.reshape(1, -1),
        donor_block.reshape(1, -1),
        panel_normals,
        observer_points,
    )
    return radiate_all(series, panel_points, observers)


def solution(mesh):
    return jax.shard_map(
        body,
        mesh=mesh,
        in_specs=(
            P("panel", None, None),
            P(("panel", "obs"), None, None),
            P(("panel", "obs"), None),
            P(("panel", "obs")),
            P(None, ("panel", "obs")),
            P(None, ("panel", "obs")),
            P(None, "obs"),
        ),
        out_specs=P("panel", "obs"),
        check_vma=False,
    )
```

time: 142 us -> 93.7 us (0.66)
  Pallas kernels: 115 us -> 89.6 us
  matrix products: 9.58 us -> 0 us
  other arithmetic: 7.43 us -> 0 us
  local copies, waits for them, and re-layouts: 8.96 us -> 3.84 us
    pallas_call x5 -> x2, Pallas kernels: 115 us -> 89.6 us  [the longest x1 46.7 us: series_all(): pl.pallas_call(functools.partial(series_kernel, share), out_shape=(jax.Sh...]
    dot_general x9 -> x0, matrix products: 9.58 us -> none  [the longest x4 5.68 us: body(): jnp.einsum('tpk,kv->tpv', weights.astype(jnp.bfloat16), arrived[:, cell *...]
    eq x5 -> x0, other arithmetic: 2.3 us -> none  [the longest x4 1.59 us: body(): cell_of == cell]
    transpose x3 -> x0, local copies, waits for them, and re-layouts: 1.94 us -> none  [the longest x2 1.67 us: body(): group[:, cut:].reshape(-1, 8, panels)[:, :3].transpose(1, 0, 2)]
    reshape x2 -> x0, local copies, waits for them, and re-layouts: 1.94 us -> none  [the longest x1 1.87 us: radiate_all(): coefs.reshape(pairs, 2 * SLOT * GROUP, 2 * orders).transpose(0, 2, 1)]
    mul x4 -> x0, other arithmetic: 1.59 us -> none  [the longest x1 1.2 us: fourier_table(): factor * jnp.cos(angles)]
    unnamed x15 -> x2, local copies, waits for them, and re-layouts: 3.27 us -> 3.84 us
where the time goes in v1:
time: 93.7 us; the launch traced here: 93.5 us
  Pallas kernels  89.6 us (96%)
  local copies, waits for them, and re-layouts  3.84 us (4%)
    pallas_call x1, Pallas kernels, series_all(): pl.pallas_call(functools.partial(series_kernel, share), out_shape=(jax.Sh...  46.7 us
    pallas_call x1, Pallas kernels, radiate_all(): pl.pallas_call(radiate_kernel, out_shape=jax.ShapeDtypeStruct((rows, coun...  42.9 us
    unnamed x2, local copies, waits for them, and re-layouts  3.84 us

profile of v1, /device:TPU:0, one launch (start us, length us, event | category | flops | bytes accessed | tf_op | source)
XLA Modules:
  0.0 93.5 jit_solution(8939482161784536821)
XLA Ops:
  0.0 2.5 %copy.11 = bf16[128,4,1280]{2,0,1:T(8,128)(2,1)} copy(bf16[128,4,1280]{2,1,0:T(4,128)(2,1)} %param.8) | data formatting | bytes 2621440 | tf_op args[0]
  2.5 46.7 %series.1 = (f32[4,256,128]{2,1,0:T(8,128)}, f32[4,3,256]{2,1,0:T(4,128)}) custom-call(bf16[4,128,1280]{2,1,0:T(8,128)(2,1)} %bitcast.6, bf16[128,512]{1,0:T(8,128)(2,1)} %bitcast.7, s32[1,128]{1,0:T(1,128)} %bitcast.8, s32[1,128]{1,0:T(1,128)} %bitcast.9, f32[3,128]{1,0:T(4,128)} %normal_ref.1, f32[3,256]{1,0:T(4,128)} %observer_ref.1), custom_call_target="tpu_custom_call" | custom-call | tf_op jit(solution)/shard_map/series/pallas_call | solution.py:296
  49.2 42.9 %radiate.1 = f32[16,256]{1,0:T(8,128)} custom-call(f32[4,256,128]{2,1,0:T(8,128)} %get-tuple-element.7.series_ref, f32[128,256]{1,0:T(8,128)} %constant.2.clone.table_ref, f32[3,128]{1,0:T(4,128)} %point_ref.1, f32[4,3,256]{2,1,0:T(4,128)} %get-tuple-element.8.observers_ref), custom_call_target="tpu_custom_call" | custom-call | tf_op jit(solution)/shard_map/radiate/pallas_call | solution.py:550
  92.1 1.3 %copy.13 = f32[16,256]{1,0:T(8,128)} copy(f32[16,256]{1,0:T(8,128)} %radiate.1) | data formatting | bytes 32768
